TPU v7x, 8 devices: a whole 2x2x1 slice. The times are simulated.
8 devices in a mesh: dp: 2 (over z, y), cp: 4 (over x, core).
Axes of the slice: x: 2, y: 2, z: 1, core: 2. Of those that a mesh axis runs over, the one named last changes fastest.
Arguments:
- x_in: bfloat16 [2, 4096, 1152], P('dp', 'cp'), parts along dimension 0
- positions: int32 [2, 4096], P('dp', 'cp'), parts along dimension 0
- dy_out: bfloat16 [2, 4096, 1152], P('dp', 'cp'), parts along dimension 0
- w_query: bfloat16 [1152, 4, 256], replicated
- w_key: bfloat16 [1152, 1, 256], replicated
- w_value: bfloat16 [1152, 1, 256], replicated
- w_out: bfloat16 [4, 256, 1152], replicated
- w_pre: float32 [1152], replicated
- w_post: float32 [1152], replicated
Outputs:
- output 1: bfloat16 [2, 4096, 1152], P('dp', 'cp'), parts along dimension 0
- output 2: bfloat16 [2, 4096, 1152], P('dp', 'cp'), parts along dimension 0
- output 3: float32 [2304, 4, 256], P('dp'), parts along dimension 0
- output 4: float32 [2304, 1, 256], P('dp'), parts along dimension 0
- output 5: float32 [2304, 1, 256], P('dp'), parts along dimension 0
- output 6: float32 [8, 256, 1152], P('dp'), parts along dimension 0
- output 7: float32 [2304], P('dp'), parts along dimension 0
- output 8: float32 [2304], P('dp'), parts along dimension 0
There are 2 independent parts. A program takes and returns all parts, laid end to end along the dimension named above; an argument that names none is the same for every part.
All inputs are finite; a program needn't handle non-finite values.
Results may differ from a plain program's by a relative error of at most 0.02.
Values are sent between devices in bfloat16 or wider.
A program may use at most 1 GiB of HBM per device.

v0:
```python
import jax
import jax.numpy as jnp
from jax import lax
from jax.experimental import pallas as pl
from jax.experimental.pallas import tpu as pltpu
from jax.sharding import PartitionSpec as P

CH = 512
H = 4
D = 256
T = 1024
NS = 8
EPS = 1e-6
ROPE_BASE = 10000.0
CAPL = 50.0*1.4426950408889634
NN = (((1,),(0,)),((),()))
NT = (((1,),(1,)),((),()))
TN = (((0,),(0,)),((),()))
F32 = jnp.float32
BF16 = jnp.bfloat16
BR = 512
PR = 256


def dot(a, b, dims=NN):
    return lax.dot_general(a, b, dims, preferred_element_type=F32)


def params(limit=44 << 20):
    return pltpu.CompilerParams(dimension_semantics=("arbitrary",), vmem_limit_bytes=limit)


def cost(us):
    return pl.CostEstimate(flops=int(us*4e7), bytes_accessed=1 << 20, transcendentals=0)


def row(i, *_):
    return (i, 0)


def const(*_):
    return (0, 0)


def whole(arr):
    return pl.BlockSpec(arr.shape, const, pipeline_mode=pl.Buffered(1))


ANY = pl.BlockSpec(memory_space=pl.ANY)


def piece_copies(kv_refs, kbuf, vbuf, sems):
    at = 0
    copies = {}
    for n, kv in enumerate(kv_refs):
        rows = kv.shape[1]
        copies[at//CH] = [pltpu.make_async_copy(kv.at[w], buf.at[pl.ds(at, rows)], sems.at[2*n+w]) for w, buf in enumerate((kbuf, vbuf))]
        at += rows
    return copies


def start_pieces(copies):
    for pair in copies.values():
        for cp in pair:
            cp.start()


def wait_pieces(copies, first, j):
    for slot, pair in copies.items():
        @pl.when(jnp.logical_and(first, j == slot))
        def _():
            for cp in pair:
                cp.wait()


def visit(ids, r, tile, begin, end=None):
    def body(j, c):
        begin(j)
        g = ids[4+j]
        @pl.when(g < r)
        def _():
            tile(j, False)
        @pl.when(g == r)
        def _():
            tile(j, True)
        if end is not None:
            end(j)
        return c
    lax.fori_loop(0, NS, body, 0)


def fwd_kernel(ids, q_ref, kv0, kv1, kv2, kv3, o_ref, ob_ref, l2_ref, kbuf, vbuf, acc, lacc, sems):
    i = pl.program_id(0)
    r = ids[i]
    copies = piece_copies((kv0, kv1, kv2, kv3), kbuf, vbuf, sems)
    @pl.when(i == 0)
    def _():
        start_pieces(copies)
    acc[...] = jnp.zeros_like(acc)
    lacc[...] = jnp.zeros_like(lacc)
    def tile(j, masked):
        at = pl.ds(pl.multiple_of(j*CH, CH), CH)
        k = kbuf[at]
        v = vbuf[at]
        n = CH//2 if masked else CH
        for h in range(H):
            for u in range(CH//n):
                rows = slice(u*n, (u+1)*n)
                cols = (u+1)*n
                e = jnp.exp2(jnp.tanh(dot(q_ref[rows, h*D:(h+1)*D], k[:cols], NT)*(1/50.0))*CAPL)
                if masked:
                    ri = lax.broadcasted_iota(jnp.int32, (n, cols), 0)+u*n
                    ci = lax.broadcasted_iota(jnp.int32, (n, cols), 1)
                    e = jnp.where(ci <= ri, e, 0.0)
                lacc[h, rows] += sum(e[:, w*128:(w+1)*128] for w in range(cols//128))
                acc[h, rows] += dot(e.astype(BF16), v[:cols])
    visit(ids, r, tile, lambda j: wait_pieces(copies, i == 0, j))
    for h in range(H):
        la = lacc[h]
        o = acc[h]/jnp.sum(la, axis=1, keepdims=True)
        o_ref[:, h*D:(h+1)*D] = o
        ob_ref[:, h*D:(h+1)*D] = o.astype(BF16)
        l2_ref[0, h:h+1, :] = jnp.log2(jnp.sum(la.T, axis=0, keepdims=True))


def flash_fwd(ids, q, kvs, us=30):
    return pl.pallas_call(
        fwd_kernel,
        grid_spec=pltpu.PrefetchScalarGridSpec(
            num_scalar_prefetch=1, grid=(2*T//CH,),
            in_specs=[pl.BlockSpec((CH, H*D), row)]+[ANY]*4,
            out_specs=[pl.BlockSpec((CH, H*D), row), pl.BlockSpec((CH, H*D), row), pl.BlockSpec((1, 8, CH), lambda i, ids: (i, 0, 0))],
            scratch_shapes=[pltpu.VMEM((NS*CH, D), BF16), pltpu.VMEM((NS*CH, D), BF16), pltpu.VMEM((H, CH, D), F32),
                            pltpu.VMEM((H, CH, 128), F32), pltpu.SemaphoreType.DMA((8,))]),
        out_shape=[jax.ShapeDtypeStruct((2*T, H*D), F32), jax.ShapeDtypeStruct((2*T, H*D), BF16), jax.ShapeDtypeStruct((4, 8, CH), F32)],
        compiler_params=params(), cost_estimate=cost(us), name="flash_fwd",
    )(ids, q, *kvs)


def bwd_kernel(ids, q_ref, do_ref, l2_ref, dlt_ref, cl_ref, sl_ref, cr_ref, sr_ref, kv0, kv1, kv2, kv3, dq_ref, own_out, sib_out,
               kbuf, vbuf, dka, dva, dqt, pt, dst, sems, fsem):
    i = pl.program_id(0)
    last = i == pl.num_programs(0)-1
    r = ids[i]
    sub = CH//2
    copies = piece_copies((kv0, kv1, kv2, kv3), kbuf, vbuf, sems)
    @pl.when(i == 0)
    def _():
        start_pieces(copies)
        dka[...] = jnp.zeros_like(dka)
        dva[...] = jnp.zeros_like(dva)
    dqt[...] = jnp.zeros_like(dqt)
    def tile(j, masked):
        at = pl.ds(pl.multiple_of(j*CH, CH), CH)
        k = kbuf[at]
        v = vbuf[at]
        kt = k.T
        steps = [(h, u) for h in range(H) for u in range(2)]
        def keys(u):
            return (u+1)*sub if masked else CH
        def score(h, u):
            rows = slice(u*sub, (u+1)*sub)
            n = keys(u)
            return dot(k[:n], q_ref[rows, h*D:(h+1)*D], NT), dot(v[:n], do_ref[rows, h*D:(h+1)*D], NT)
        def soft(sd, h, u):
            s, dp = sd
            n = keys(u)
            rows = slice(u*sub, (u+1)*sub)
            t = jnp.tanh(s*(1/50.0))
            p = jnp.exp2(t*CAPL-l2_ref[0, h:h+1, rows])
            if masked:
                ki = lax.broadcasted_iota(jnp.int32, (n, sub), 0)
                qi = lax.broadcasted_iota(jnp.int32, (n, sub), 1)+u*sub
                p = jnp.where(ki <= qi, p, 0.0)
            ds = (p*(dp-dlt_ref[0, h:h+1, rows])*(1.0-t*t)).astype(BF16)
            c0 = h*CH+u*sub
            pt[:n, c0:c0+sub] = p.astype(BF16)
            dst[:n, c0:c0+sub] = ds
            if n < CH:
                pt[n:, c0:c0+sub] = jnp.zeros((CH-n, sub), BF16)
                dst[n:, c0:c0+sub] = jnp.zeros((CH-n, sub), BF16)
            return ds
        def dqs(ds, h, u):
            c0 = h*CH+u*sub
            dqt[:, c0:c0+sub] += dot(kt[:, :keys(u)], ds)
        def dkv_head(h):
            dva[at] += dot(pt[:, h*CH:(h+1)*CH], do_ref[:, h*D:(h+1)*D])
            dka[at] += dot(dst[:, h*CH:(h+1)*CH], q_ref[:, h*D:(h+1)*D])
        n = len(steps)
        s = score(*steps[0])
        e = None
        for m in range(n):
            s2 = score(*steps[m+1]) if m+1 < n else None
            e2 = soft(s, *steps[m])
            if e is not None:
                dqs(e, *steps[m-1])
            if m and m % 2 == 0:
                dkv_head(m//2-1)
            s, e = s2, e2
        dqs(e, *steps[n-1])
        dkv_head(H-1)
    def flush(j):
        at = pl.ds(pl.multiple_of(j*CH, CH), CH)
        @pl.when(jnp.logical_and(last, j < NS//2))
        def _():
            pltpu.make_async_copy(dka.at[at], own_out.at[0, at], fsem.at[0]).start()
            pltpu.make_async_copy(dva.at[at], own_out.at[1, at], fsem.at[1]).start()
        @pl.when(jnp.logical_and(last, j >= NS//2))
        def _():
            to = pl.ds(pl.multiple_of(j*CH-2*T, CH), CH)
            pltpu.make_async_copy(dka.at[at], sib_out.at[0, to], fsem.at[2]).start()
            pltpu.make_async_copy(dva.at[at], sib_out.at[1, to], fsem.at[3]).start()
    visit(ids, r, tile, lambda j: wait_pieces(copies, i == 0, j), flush)
    left = i < T//CH
    c = jnp.where(left, cl_ref[...], cr_ref[...])
    s = jnp.where(left, sl_ref[...], sr_ref[...])
    for h in range(H):
        x = dqt[:, h*CH:(h+1)*CH].T
        a = x[:, :128]
        b = x[:, 128:]
        dq_ref[:, h*D:h*D+128] = ((a*c+b*s)*(1/12.0)).astype(BF16)
        dq_ref[:, h*D+128:(h+1)*D] = ((b*c-a*s)*(1/12.0)).astype(BF16)
    @pl.when(last)
    def _():
        lo = pl.ds(0, 2*T)
        hi = pl.ds(2*T, 2*T)
        pltpu.make_async_copy(dka.at[lo], own_out.at[0], fsem.at[0]).wait()
        pltpu.make_async_copy(dva.at[lo], own_out.at[1], fsem.at[1]).wait()
        pltpu.make_async_copy(dka.at[hi], sib_out.at[0], fsem.at[2]).wait()
        pltpu.make_async_copy(dva.at[hi], sib_out.at[1], fsem.at[3]).wait()


def flash_bwd(ids, q, do, l2, dlt, cl, sl, cr, sr, kvs, us=70):
    n = T//CH
    big = pl.BlockSpec((CH, H*D), row)
    stat = pl.BlockSpec((1, 8, CH), lambda i, ids: (i, 0, 0))
    left = pl.BlockSpec((CH, 128), lambda i, ids: (jnp.minimum(i, n-1), 0))
    right = pl.BlockSpec((CH, 128), lambda i, ids: (jnp.maximum(i-n, 0), 0))
    return pl.pallas_call(
        bwd_kernel,
        grid_spec=pltpu.PrefetchScalarGridSpec(
            num_scalar_prefetch=1, grid=(2*n,),
            in_specs=[big, big, stat, stat, left, left, right, right]+[ANY]*4,
            out_specs=[big, ANY, ANY],
            scratch_shapes=[pltpu.VMEM((NS*CH, D), BF16), pltpu.VMEM((NS*CH, D), BF16), pltpu.VMEM((NS*CH, D), F32), pltpu.VMEM((NS*CH, D), F32),
                            pltpu.VMEM((D, H*CH), F32), pltpu.VMEM((CH, H*CH), BF16), pltpu.VMEM((CH, H*CH), BF16),
                            pltpu.SemaphoreType.DMA((8,)), pltpu.SemaphoreType.DMA((4,))]),
        out_shape=[jax.ShapeDtypeStruct((2*T, H*D), BF16)]+[jax.ShapeDtypeStruct((2, 2*T, D), F32)]*2,
        compiler_params=params(), cost_estimate=cost(us), name="flash_bwd",
    )(ids, q, do, l2, dlt, cl, sl, cr, sr, *kvs)


def proj_kernel(*refs):
    x_ref, cos_ref, sin_ref, wp_ref, wq_ref, wk_ref, wv_ref = refs[:7]
    a_ref, q_ref, kv_ref = refs[-3:]
    x = x_ref[...].astype(F32)
    rinv = lax.rsqrt(jnp.mean(x*x, axis=-1, keepdims=True)+EPS)
    a = (x*rinv*(1.0+wp_ref[...])).astype(BF16)
    a_ref[...] = a.T
    c = cos_ref[...]
    s = sin_ref[...]
    def rope(y, scale):
        y = y.astype(BF16).astype(F32)
        f = y[:, :128]
        g = y[:, 128:]
        return ((f*c-g*s)*scale).astype(BF16), ((g*c+f*s)*scale).astype(BF16)
    for h in range(H):
        f, g = rope(dot(a, wq_ref[:, h*D:(h+1)*D]), 1/12.0)
        q_ref[:, h*D:h*D+128] = f
        q_ref[:, h*D+128:(h+1)*D] = g
    f, g = rope(dot(a, wk_ref[...]), 1.0)
    kv_ref[0, :, :128] = f
    kv_ref[0, :, 128:] = g
    kv_ref[1] = dot(a, wv_ref[...]).astype(BF16)


def proj(x, cos, sin, wp, wq, wk, wv, prev=(), at=0):
    rows, m = x.shape
    t = T
    n = rows//PR
    return pl.pallas_call(
        proj_kernel, grid=(n,),
        in_specs=[pl.BlockSpec((PR, m), row), pl.BlockSpec((PR, 128), row), pl.BlockSpec((PR, 128), row), pl.BlockSpec((1, m), const),
                  whole(wq), whole(wk), whole(wv)]+[ANY]*len(prev),
        out_specs=[pl.BlockSpec((m, PR), lambda i: (0, i+at*(BR//PR))), pl.BlockSpec((PR, H*D), lambda i: (i+at*(BR//PR), 0)), pl.BlockSpec((2, PR, D), lambda i: (0, i, 0))],
        out_shape=[jax.ShapeDtypeStruct((m, 2*t), BF16), jax.ShapeDtypeStruct((2*t, H*D), BF16), jax.ShapeDtypeStruct((2, rows, D), BF16)],
        input_output_aliases={7: 0, 8: 1} if prev else {},
        compiler_params=params(44 << 20), cost_estimate=cost(8), name="proj",
    )(x, cos, sin, wp, wq, wk, wv, *prev)


def post_kernel(ob_ref, o_ref, wp_ref, wo_ref, x_ref, dyl_ref, dyr_ref, y_ref, do_ref, dlt_ref, dwo_ref, dwp_ref, dzs):
    i = pl.program_id(0)
    left = i < T//BR
    sub = 256
    n = BR//sub
    @pl.when(i == 0)
    def _():
        dwp_ref[...] = jnp.zeros_like(dwp_ref)
        dwo_ref[...] = jnp.zeros_like(dwo_ref)
    gain = 1.0+wp_ref[...]
    def part(u):
        return slice(u*sub, (u+1)*sub)
    def first(u):
        return dot(ob_ref[part(u)], wo_ref[...]).astype(BF16)
    def middle(z, u):
        z = z.astype(F32)
        rinv = lax.rsqrt(jnp.mean(z*z, axis=-1, keepdims=True)+EPS)
        zh = z*rinv
        dy = jnp.where(left, dyl_ref[part(u)].astype(F32), dyr_ref[part(u)].astype(F32))
        y = (x_ref[part(u)].astype(F32)+(zh*gain).astype(BF16).astype(F32)).astype(BF16)
        y_ref[part(u)] = jnp.where(left, y, y_ref[part(u)])
        dwp_ref[...] += jnp.where(left, jnp.sum(dy*zh, axis=0, keepdims=True), 0.0)
        g = dy*gain
        dz = (rinv*(g-zh*jnp.mean(g*zh, axis=-1, keepdims=True))).astype(BF16)
        dzs[part(u)] = dz
        return dz
    def second(dz, u):
        do = dot(dz, wo_ref[...], NT).astype(BF16)
        do_ref[part(u)] = do
        for h in range(H):
            w = do[:, h*D:(h+1)*D].astype(F32)*o_ref[part(u), h*D:(h+1)*D]
            dlt_ref[0, h:h+1, part(u)] = jnp.sum((w[:, :128]+w[:, 128:]).T, axis=0, keepdims=True)
    z = first(0)
    dz = None
    for u in range(n):
        z2 = first(u+1) if u+1 < n else None
        dz2 = middle(z, u)
        if dz is not None:
            second(dz, u-1)
        z, dz = z2, dz2
    second(dz, n-1)
    dwo_ref[...] += dot(ob_ref[...], dzs[...], TN)


def post(ob, o, x, dyl, dyr, wp, wo):
    t, m = x.shape
    n = t//BR
    spec = pl.BlockSpec((BR, m), lambda i: (jnp.minimum(i, n-1), 0))
    right = pl.BlockSpec((BR, m), lambda i: (jnp.maximum(i-n, 0), 0))
    big = pl.BlockSpec((BR, H*D), row)
    return pl.pallas_call(
        post_kernel, grid=(2*n,),
        in_specs=[big, big, pl.BlockSpec((1, m), const), whole(wo), spec, spec, right],
        out_specs=[spec, big, pl.BlockSpec((1, 8, CH), lambda i: (i, 0, 0)), pl.BlockSpec((H*D, m), const), pl.BlockSpec((1, m), const)],
        scratch_shapes=[pltpu.VMEM((BR, m), BF16)],
        out_shape=[jax.ShapeDtypeStruct((t, m), BF16), jax.ShapeDtypeStruct((2*t, H*D), BF16), jax.ShapeDtypeStruct((4, 8, CH), F32),
                   jax.ShapeDtypeStruct((H*D, m), F32), jax.ShapeDtypeStruct((1, m), F32)],
        compiler_params=params(), cost_estimate=cost(25), name="post",
    )(ob, o, wp, wo, x, dyl, dyr)


def rope_back(dk, c, s, scale):
    f = dk[:, :128]
    g = dk[:, 128:]
    return jnp.concatenate([(f*c+g*s)*scale, (g*c-f*s)*scale], axis=1).astype(BF16)


def final_kernel(at_h, dq_h, own_h, sib_h, x_h, dy_h, cl_h, sl_h, cr_h, sr_h, wq_h, wk_h, wv_h, wp_ref, gp_ref, q_out, kv_out, dx_out, gain_ref,
                 at, dq, own, got, x, dy, cl, sl, cr, sr, wq, wk, wv, q_own, q_in, kv_own, kv_in, dkv, dx, gbuf, gin, lsem, osem, ssem, rsem):
    idx = lax.axis_index("cp")
    peers = (idx+1-2*lax.rem(idx, 2), lax.rem(idx+2, 4), 3-idx)
    barrier = pltpu.get_barrier_semaphore()
    for p in peers:
        pl.semaphore_signal(barrier, inc=1, device_id={"cp": p}, device_id_type=pl.DeviceIdType.MESH)

    def remote(src, dst, n, p=0):
        return pltpu.make_async_remote_copy(src_ref=src, dst_ref=dst, send_sem=ssem.at[n], recv_sem=rsem.at[n], device_id={"cp": peers[p]},
                                            device_id_type=pl.DeviceIdType.MESH)

    pairs = [(at_h, at)]+[(dq_h.at[:, pl.ds(h*D, D)], dq.at[h]) for h in range(H)]+[(own_h, own), (cl_h, cl), (sl_h, sl), (cr_h, cr), (sr_h, sr),
             (wq_h, wq), (wk_h, wk), (wv_h, wv), (x_h, x), (dy_h, dy)]
    loads = [pltpu.make_async_copy(a, b, lsem.at[n]) for n, (a, b) in enumerate(pairs)]
    for cp in loads:
        cp.start()
    pl.semaphore_wait(barrier, 3)
    kv_got = remote(sib_h, got, 0)
    kv_got.start()
    def q_send(h):
        return remote(q_own.at[h], q_in.at[h], 1+h)
    loads[0].wait()
    def q_block(h, c):
        pltpu.make_async_copy(dq_h.at[:, pl.ds(pl.multiple_of(h*D, D), D)], dq.at[h], lsem.at[1+h]).wait()
        q_own[h] = dot(at[...], dq[h])
        @pl.when(h > 0)
        def _():
            q_send(h-1).start()
        return c
    lax.fori_loop(0, H, q_block, 0)
    for cp in loads[5:10]:
        cp.wait()
    kv_got.wait()
    for b in range(4):
        rows = slice(b*CH, (b+1)*CH)
        c, s = (cl, sl) if b < 2 else (cr, sr)
        tab = slice((b % 2)*CH, (b % 2+1)*CH)
        dkv[rows, :D] = rope_back(own[0, rows]+got[0, rows], c[tab], s[tab], 1.0)
        dkv[rows, D:] = (own[1, rows]+got[1, rows]).astype(BF16)
    q_send(H-1).start()
    kv_own[...] = dot(at[...], dkv[...])
    kv_send = remote(kv_own, kv_in, 5)
    for cp in loads[10:]:
        cp.wait()
    gbuf[...] = jnp.zeros_like(gbuf)
    kv_send.start()
    def dx_block(b, c):
        rows = pl.ds(pl.multiple_of(b*CH, CH), CH)
        da = dot(dkv[rows, :D], wk[...], NT)+dot(dkv[rows, D:], wv[...], NT)
        for h in range(H):
            da += dot(dq[h, rows], wq[:, h*D:(h+1)*D], NT)
        xv = x[rows].astype(F32)
        rinv = lax.rsqrt(jnp.mean(xv*xv, axis=-1, keepdims=True)+EPS)
        xh = xv*rinv
        gbuf[0:1] += jnp.sum(da*xh, axis=0, keepdims=True)
        g = da*(1.0+wp_ref[...])
        dx[rows] = (dy[rows].astype(F32)+rinv*(g-xh*jnp.mean(g*xh, axis=-1, keepdims=True))).astype(BF16)
        return c
    lax.fori_loop(0, T//CH, dx_block, 0)
    gbuf[1:2] = gp_ref[...]
    outs = [pltpu.make_async_copy(dx, dx_out, osem.at[0])]
    outs[0].start()
    g_sends = [remote(gbuf, gin.at[p], 6+p, p) for p in range(3)]
    def q_sum(h, c):
        q_send(h).wait()
        q_own[h] += q_in[h]
        pltpu.make_async_copy(q_own.at[h], q_out.at[h], osem.at[1+h]).start()
        @pl.when(h == 0)
        def _():
            for cp in g_sends:
                cp.start()
        return c
    lax.fori_loop(0, H, q_sum, 0)
    outs += [pltpu.make_async_copy(q_own.at[h], q_out.at[h], osem.at[1+h]) for h in range(H)]
    kv_send.wait()
    kv_own[...] += kv_in[...]
    cp = pltpu.make_async_copy(kv_own, kv_out, osem.at[5])
    cp.start()
    outs.append(cp)
    for cp in g_sends:
        cp.wait()
    gain_ref[...] = (gbuf[...]+gin[0])+(gin[1]+gin[2])
    for cp in outs:
        cp.wait()


def final(at, dq, own, sib, x, dy, cl, sl, cr, sr, wq, wk, wv, wp, gp):
    t, m = x.shape
    vm = pl.BlockSpec(memory_space=pltpu.VMEM)
    V = pltpu.VMEM
    DMA = pltpu.SemaphoreType.DMA
    tab = V((t, 128), F32)
    return pl.pallas_call(
        final_kernel,
        in_specs=[ANY]*13+[vm, vm],
        out_specs=[ANY, ANY, ANY, vm],
        out_shape=[jax.ShapeDtypeStruct((H, m, D), F32), jax.ShapeDtypeStruct((m, 2*D), F32), jax.ShapeDtypeStruct((t, m), BF16), jax.ShapeDtypeStruct((8, m), F32)],
        scratch_shapes=[V((m, 2*t), BF16), V((H, 2*t, D), BF16), V((2, 2*t, D), F32), V((2, 2*t, D), F32), V((t, m), BF16), V((t, m), BF16), tab, tab, tab, tab,
                        V(wq.shape, BF16), V(wk.shape, BF16), V(wv.shape, BF16), V((H, m, D), F32), V((H, m, D), F32), V((m, 2*D), F32), V((m, 2*D), F32),
                        V((2*t, 2*D), BF16), V((t, m), BF16), V((8, m), F32), V((3, 8, m), F32), DMA((15,)), DMA((6,)), DMA((9,)), DMA((9,))],
        compiler_params=pltpu.CompilerParams(collective_id=0, has_side_effects=True, vmem_limit_bytes=67043328),
        cost_estimate=cost(20), name="final",
    )(at, dq, own, sib, x, dy, cl, sl, cr, sr, wq, wk, wv, wp, gp)


def relay_kernel(q_ref, kv_ref, o0, o1, dq_ref, dk_ref, dv_ref, do_ref):
    for h in range(H):
        dq_ref[:, h, :] = q_ref[h]
    dk_ref[:, 0, :] = kv_ref[:, :D]
    dv_ref[:, 0, :] = kv_ref[:, D:]
    do_ref[...] = o0[...]+o1[...]


def relay(q, kv, o0, o1, n=4):
    m = kv.shape[0]
    rows = m//n
    out = lambda e: pl.BlockSpec((rows, e, D), lambda i: (i, 0, 0))
    side = pl.BlockSpec((H*D//n, m), row)
    return pl.pallas_call(
        relay_kernel, grid=(n,),
        in_specs=[pl.BlockSpec((H, rows, D), lambda i: (0, i, 0)), pl.BlockSpec((rows, 2*D), row), side, side],
        out_specs=[out(H), out(1), out(1), side],
        out_shape=[jax.ShapeDtypeStruct((m, e, D), F32) for e in (H, 1, 1)]+[jax.ShapeDtypeStruct((H*D, m), F32)],
        compiler_params=params(60 << 20), cost_estimate=cost(9), name="relay",
    )(q, kv, o0, o1)


def tables(pos):
    inv = ROPE_BASE ** (jnp.arange(128, dtype=F32)*(-2.0/256))
    ang = pos.astype(F32)[:, None]*inv
    return jnp.cos(ang), jnp.sin(ang)


def solution(mesh):
    def local_step(x_in, positions, dy_out, w_query, w_key, w_value, w_out, w_pre, w_post):
        m = x_in.shape[2]
        x = x_in[0]
        dy = dy_out[0]
        wq = w_query.reshape(m, H*D)
        wk = w_key.reshape(m, D)
        wv = w_value.reshape(m, D)
        wo = w_out.reshape(H*D, m)
        wpre = w_pre.reshape(1, m)
        wpost = w_post.reshape(1, m)
        idx = lax.axis_index("cp")

        def swap(v, mask):
            return lax.ppermute(v, "cp", [(i, i ^ mask) for i in range(4)])

        order = (0, 3, 1, 2)
        ids = jnp.stack([2*(idx ^ g)+e for g in (0, 3)+order for e in range(2)]).astype(jnp.int32)

        def send(v):
            return swap(v, 3)

        pr = send(positions[0])
        xr = send(x)
        dyr = send(dy)
        cl, sl = tables(positions[0])
        at, q, kvl = proj(x, cl, sl, wpre, wq, wk, wv)
        kvs = swap(kvl, 1)
        pr = lax.optimization_barrier((pr, kvl))[0]
        cr, sr = tables(pr)
        at, q, kvr = proj(xr, cr, sr, wpre, wq, wk, wv, prev=(at, q), at=2)
        kvrs = swap(kvr, 1)
        kv4 = (kvl, kvr, kvs, kvrs)
        o, ob, l2 = flash_fwd(ids, q, kv4)
        y, do, dlt, dwo, dwpost = post(ob, o, x, dy, dyr, wpost, wo)
        dwo_in = swap(dwo, 1)
        dq, own, sib = flash_bwd(ids, q, do, l2, dlt, cl, sl, cr, sr, kv4)

        dwq, dwkv, dx, gains = final(at, dq, own, sib, x, dy, cl, sl, cr, sr, wq, wk, wv, wpre, dwpost)
        dwq, dwk, dwv, dwo = relay(dwq, dwkv, dwo, dwo_in)
        return (y[None], dx[None], dwq, dwk, dwv, dwo.reshape(H, D, m), gains[0], gains[1])

    seq = P("dp", "cp", None)
    in_specs = (seq, P("dp", "cp"), seq, P(), P(), P(), P(), P(), P())
    out_specs = (seq, seq, P("dp", None, None), P("dp", None, None), P("dp", None, None), P("dp", None, None), P("dp"), P("dp"))
    return jax.shard_map(local_step, mesh=mesh, in_specs=in_specs, out_specs=out_specs, check_vma=False)
```

profile of v0, /device:TPU:0, one launch (start us, length us, event | category | flops | bytes accessed | tf_op | source)
XLA Modules:
  0.0 291.2 jit_solution(17814550016382035094)
XLA Ops:
  0.6 0.0 copy-start.1
  0.6 0.0 copy-start.10
  0.7 0.0 copy-start.9
  0.7 2.8 collective-permute-start
  3.4 0.0 collective-permute-start.4
  3.5 1.7 collective-permute-start.1
  5.2 0.7 convert_element_type.10
  5.9 0.7 reshape.48.refs_3_.wp_ref
  6.6 0.0 copy-start.13
  6.6 2.2 copy.19
  8.8 0.0 copy-start
  8.9 1.9 multiply_sine_fusion.1
  10.8 0.0 copy-start.3
  10.8 0.0 copy-start.4
  10.8 0.0 copy-done.1
  10.8 0.0 copy-done.10
  10.8 0.0 copy-done.9
  10.8 6.7 %proj.2 = (bf16[1152,2048]{1,0:T(8,128)(2,1)}, bf16[2048,1024]{1,0:T(8,128)(2,1)}, bf16[2,1024,256]{2,1,0:T(8,128)(2,1)}) custom-call(bf16[1024,1152]{1,0:T(8,128)(2,1)S(1)} %bitcast.24, f32[1024,128]{1,0:T(8,128)S(1)} %get-tuple-element.65.refs_1_.cl_ref.cl_h, f32[1024,128]{1,0:T(8,128)S(1)} %get-tuple-element.64.refs_2_.sl_ref.sl_h, ...), custom_call_target="tpu_custom_call" | custom-call | flops 320000000 | bytes 1048576 | tf_op jit(solution)/shard_map/proj/pallas_call | solution.py:281
  17.5 0.7 collective-permute-start.2
  18.2 87.8 %collective-permute-done.1 = s32[1024]{0:T(1024)S(1)} collective-permute-done((s32[1024]{0:T(1024)}, s32[1024]{0:T(1024)S(1)}, u32[]{:S(2)}, u32[]{:S(2)}) %collective-permute-start.1) | collective-permute-done | bytes 4128 | tf_op jit(solution)/shard_map/ppermute | solution.py:507
  106.0 1.9 multiply_sine_fusion
  107.8 0.0 copy-start.5
  107.9 0.0 copy-start.7
  107.9 0.0 collective-permute-done.refs_0_
  107.9 0.0 copy-done.13
  107.9 0.0 copy-done
  107.9 0.0 copy-start.16
  107.9 6.7 %proj.3 = (bf16[1152,2048]{1,0:T(8,128)(2,1)}, bf16[2048,1024]{1,0:T(8,128)(2,1)}, bf16[2,1024,256]{2,1,0:T(8,128)(2,1)}) custom-call(bf16[1024,1152]{1,0:T(8,128)(2,1)S(1)} %collective-permute-done.refs_0_, f32[1024,128]{1,0:T(8,128)S(1)} %get-tuple-element.63.refs_1_.cr_ref.cr_h, ...), custom_call_target="tpu_custom_call", output_to_operand_aliasing={{0}: (7, {}), {1}: (8, {})} | custom-call | flops 320000000 | bytes 1048576 | tf_op jit(solution)/shard_map/proj/pallas_call | solution.py:281
  114.6 0.0 copy-done.5
  114.6 0.0 copy-done.7
  114.6 0.1 collective-permute-start.3
  114.7 0.0 copy-done.16
  114.7 0.1 stack.39.ids
  114.8 0.0 collective-permute-done.2.kv2
  114.8 2.8 collective-permute-done.3.kv3
  117.6 0.0 copy-start.2
  117.6 0.0 copy-start.12
  117.6 34.8 %flash_fwd.1 = (f32[2048,1024]{1,0:T(8,128)}, bf16[2048,1024]{1,0:T(8,128)(2,1)S(1)}, f32[4,8,512]{2,1,0:T(8,128)S(1)}) custom-call(s32[12]{0:T(128)S(1)} %stack.39.ids, bf16[2048,1024]{1,0:T(8,128)(2,1)} %get-tuple-element.38.q_ref, bf16[2,1024,256]{2,1,0:T(8,128)(2,1)} %get-tuple-element.34.kv0, bf16[2,1024,256]{2,1,0:T(8,128)(2,1)} %get-tuple-element.39.kv1, ...), custom_call_target="tpu_custom_call" | custom-call | flops 1200000000 | bytes 1048576 | tf_op jit(solution)/shard_map/flash_fwd/pallas_call | solution.py:127
  152.4 0.0 copy-start.11
  152.4 2.0 copy-done.11
  154.4 0.0 collective-permute-done.4.dyr_ref
  154.4 0.0 copy-done.2
  154.4 0.0 copy-done.12
  154.4 0.0 copy-start.6
  154.4 0.0 copy-start.8
  154.4 28.0 %post.1 = (bf16[1024,1152]{1,0:T(8,128)(2,1)}, bf16[2048,1024]{1,0:T(8,128)(2,1)}, f32[4,8,512]{2,1,0:T(8,128)S(1)}, f32[1024,1152]{1,0:T(8,128)}, f32[1,1152]{1,0:T(1,128)S(1)}) custom-call(bf16[2048,1024]{1,0:T(8,128)(2,1)} %copy-done.11, f32[2048,1024]{1,0:T(8,128)} %get-tuple-element.41.o_ref, f32[1,1152]{1,0:T(1,128)S(1)} %reshape.52.wp_ref, ...), custom_call_target="tpu_custom_call" | custom-call | flops 1000000000 | bytes 1048576 | tf_op jit(solution)/shard_map/post/pallas_call | solution.py:342
  182.4 0.0 copy-start.14
  182.5 0.1 collective-permute-start.5
  182.6 0.0 copy-done.3
  182.6 0.0 copy-done.4
  182.6 0.0 copy-done.6
  182.6 0.0 copy-done.8
  182.6 68.9 %flash_bwd.1 = (bf16[2048,1024]{1,0:T(8,128)(2,1)}, f32[2,2048,256]{2,1,0:T(8,128)}, f32[2,2048,256]{2,1,0:T(8,128)}) custom-call(s32[12]{0:T(128)S(1)} %stack.39.ids, bf16[2048,1024]{1,0:T(8,128)(2,1)} %get-tuple-element.38.q_ref, bf16[2048,1024]{1,0:T(8,128)(2,1)} %get-tuple-element.44.do_ref, f32[4,8,512]{2,1,0:T(8,128)S(1)} %get-tuple-element.45.l2_ref, ...), custom_call_target="tpu_custom_call" | custom-call | flops 2800000000 | bytes 1048576 | tf_op jit(solution)/shard_map/flash_bwd/pallas_call | solution.py:239
  251.5 0.0 copy-done.14
  251.5 26.0 %final.1 = (f32[4,1152,256]{2,1,0:T(8,128)}, f32[1152,512]{1,0:T(8,128)}, bf16[1024,1152]{1,0:T(8,128)(2,1)}, f32[8,1152]{1,0:T(8,128)}) custom-call(bf16[1152,2048]{1,0:T(8,128)(2,1)} %get-tuple-element.43.at_h, bf16[2048,1024]{1,0:T(8,128)(2,1)} %get-tuple-element.47.dq_h, f32[2,2048,256]{2,1,0:T(8,128)} %get-tuple-element.48.own_h, ...), custom_call_target="tpu_custom_call" | custom-call | flops 800000000 | bytes 1048576 | tf_op jit(solution)/shard_map/final/pallas_call | solution.py:452
  277.5 1.5 slice_reduce_fusion
  279.0 0.0 collective-permute-done.5.o1
  279.0 0.0 copy-start.15
  279.0 10.8 %relay.1 = (f32[1152,4,256]{2,1,0:T(4,128)}, f32[1152,1,256]{2,1,0:T(1,128)}, f32[1152,1,256]{2,1,0:T(1,128)}, f32[1024,1152]{1,0:T(8,128)}) custom-call(f32[4,1152,256]{2,1,0:T(8,128)} %get-tuple-element.52.q_ref, f32[1152,512]{1,0:T(8,128)} %get-tuple-element.53.kv_ref, f32[1024,1152]{1,0:T(8,128)} %get-tuple-element.54.o0, ...), custom_call_target="tpu_custom_call" | custom-call | flops 360000000 | bytes 1048576 | tf_op jit(solution)/shard_map/relay/pallas_call | solution.py:478
  289.8 0.0 copy-done.15
  289.8 1.4 copy.23
  (3 shorter events, 0.0 us)
Async XLA Ops:
  0.6 10.2 %copy-start.1 = (bf16[1,1024,1152]{2,1,0:T(8,128)(2,1)S(1)}, bf16[1,1024,1152]{2,1,0:T(8,128)(2,1)}, u32[]{:S(2)}) copy-start(bf16[1,1024,1152]{2,1,0:T(8,128)(2,1)} %param.9) | copy-start | bytes 7077892
  0.6 10.1 %copy-start.10 = (bf16[1152,1,256]{2,0,1:T(8,128)(2,1)S(1)}, bf16[1152,1,256]{2,0,1:T(8,128)(2,1)}, u32[]{:S(2)}) copy-start(bf16[1152,1,256]{2,0,1:T(8,128)(2,1)} %param.14) | copy-start | bytes 1769476
  0.7 10.1 %copy-start.9 = (bf16[1152,1,256]{2,0,1:T(8,128)(2,1)S(1)}, bf16[1152,1,256]{2,0,1:T(8,128)(2,1)}, u32[]{:S(2)}) copy-start(bf16[1152,1,256]{2,0,1:T(8,128)(2,1)} %param.13) | copy-start | bytes 1769476
  0.7 107.2 %collective-permute-start = (bf16[1024,1152]{1,0:T(8,128)(2,1)}, bf16[1024,1152]{1,0:T(8,128)(2,1)S(1)}, u32[]{:S(2)}, u32[]{:S(2)}) collective-permute-start(bf16[1024,1152]{1,0:T(8,128)(2,1)} %bitcast.22), channel_id=1, source_target_pairs={{0,3},{1,2},{2,1},{3,0},{4,7},{5,6},{6,5},{7,4}} | collective-permute-start | bytes 7077896 | tf_op jit(solution)/shard_map/ppermute | solution.py:507
  3.4 151.0 %collective-permute-start.4 = (bf16[1024,1152]{1,0:T(8,128)(2,1)}, bf16[1024,1152]{1,0:T(8,128)(2,1)}, u32[]{:S(2)}, u32[]{:S(2)}) collective-permute-start(bf16[1024,1152]{1,0:T(8,128)(2,1)} %bitcast.26), channel_id=1, source_target_pairs={{0,3},{1,2},{2,1},{3,0},{4,7},{5,6},{6,5},{7,4}} | collective-permute-start | bytes 7077896 | tf_op jit(solution)/shard_map/ppermute | solution.py:507
  3.5 102.5 %collective-permute-start.1 = (s32[1024]{0:T(1024)}, s32[1024]{0:T(1024)S(1)}, u32[]{:S(2)}, u32[]{:S(2)}) collective-permute-start(s32[1024]{0:T(1024)} %bitcast.38), channel_id=1, source_target_pairs={{0,3},{1,2},{2,1},{3,0},{4,7},{5,6},{6,5},{7,4}} | collective-permute-start | bytes 12296 | tf_op jit(solution)/shard_map/ppermute | solution.py:507
  6.6 101.3 %copy-start.13 = (f32[1,1152]{1,0:T(1,128)}, f32[1,1152]{1,0:T(1,128)S(1)}, u32[]{:S(2)}) copy-start(f32[1,1152]{1,0:T(1,128)S(1)} %reshape.48.refs_3_.wp_ref) | copy-start | bytes 13828
  8.8 99.0 %copy-start = (bf16[144,8,4,256]{3,1,2,0:T(8,128)(2,1)}, bf16[144,8,4,256]{3,1,2,0:T(8,128)(2,1)S(1)}, u32[]{:S(2)}) copy-start(bf16[144,8,4,256]{3,1,2,0:T(8,128)(2,1)S(1)} %copy.19) | copy-start | bytes 7077892
  10.8 171.8 %copy-start.3 = (f32[1024,128]{1,0:T(8,128)}, f32[1024,128]{1,0:T(8,128)S(1)}, u32[]{:S(2)}) copy-start(f32[1024,128]{1,0:T(8,128)S(1)} %get-tuple-element.64.refs_2_.sl_ref.sl_h) | copy-start | bytes 1572868
  10.8 171.8 %copy-start.4 = (f32[1024,128]{1,0:T(8,128)}, f32[1024,128]{1,0:T(8,128)S(1)}, u32[]{:S(2)}) copy-start(f32[1024,128]{1,0:T(8,128)S(1)} %get-tuple-element.65.refs_1_.cl_ref.cl_h) | copy-start | bytes 1572868
  17.5 97.3 %collective-permute-start.2 = (bf16[2,1024,256]{2,1,0:T(8,128)(2,1)}, bf16[2,1024,256]{2,1,0:T(8,128)(2,1)}, u32[]{:S(2)}, u32[]{:S(2)}) collective-permute-start(bf16[2,1024,256]{2,1,0:T(8,128)(2,1)} %get-tuple-element.34.kv0), channel_id=1, source_target_pairs={{0,1},{1,0},{2,3},{3,2},{4,5},{5,4},{6,7},{7,6}} | collective-permute-start | bytes 3145736 | tf_op jit(solution)/shard_map/ppermute | solution.py:507
  107.8 6.8 %copy-start.5 = (f32[1024,128]{1,0:T(8,128)}, f32[1024,128]{1,0:T(8,128)S(1)}, u32[]{:S(2)}) copy-start(f32[1024,128]{1,0:T(8,128)S(1)} %get-tuple-element.62.refs_2_.sr_ref.sr_h) | copy-start | bytes 1572868
  107.9 6.8 %copy-start.7 = (f32[1024,128]{1,0:T(8,128)}, f32[1024,128]{1,0:T(8,128)S(1)}, u32[]{:S(2)}) copy-start(f32[1024,128]{1,0:T(8,128)S(1)} %get-tuple-element.63.refs_1_.cr_ref.cr_h) | copy-start | bytes 1572868
  107.9 6.8 %copy-start.16 = (f32[1152]{0:T(1024)S(1)}, f32[1152]{0:T(1024)}, u32[]{:S(2)}) copy-start(f32[1152]{0:T(1024)} %param.17) | copy-start | bytes 13828
  114.6 3.0 %collective-permute-start.3 = (bf16[2,1024,256]{2,1,0:T(8,128)(2,1)}, bf16[2,1024,256]{2,1,0:T(8,128)(2,1)}, u32[]{:S(2)}, u32[]{:S(2)}) collective-permute-start(bf16[2,1024,256]{2,1,0:T(8,128)(2,1)} %get-tuple-element.39.kv1), channel_id=1, source_target_pairs={{0,1},{1,0},{2,3},{3,2},{4,5},{5,4},{6,7},{7,6}} | collective-permute-start | bytes 3145736 | tf_op jit(solution)/shard_map/ppermute | solution.py:507
  117.6 36.8 %copy-start.2 = (bf16[1,1024,1152]{2,1,0:T(8,128)(2,1)S(1)}, bf16[1,1024,1152]{2,1,0:T(8,128)(2,1)}, u32[]{:S(2)}) copy-start(bf16[1,1024,1152]{2,1,0:T(8,128)(2,1)} %param.11) | copy-start | bytes 7077892
  117.6 36.8 %copy-start.12 = (bf16[4,256,1152]{2,1,0:T(8,128)(2,1)S(1)}, bf16[4,256,1152]{2,1,0:T(8,128)(2,1)}, u32[]{:S(2)}) copy-start(bf16[4,256,1152]{2,1,0:T(8,128)(2,1)} %param.15) | copy-start | bytes 7077892
  152.4 2.0 copy-start.11
  154.4 28.2 %copy-start.6 = (f32[1024,128]{1,0:T(8,128)S(1)}, f32[1024,128]{1,0:T(8,128)}, u32[]{:S(2)}) copy-start(f32[1024,128]{1,0:T(8,128)} %copy-done.5) | copy-start | bytes 1572868
  154.4 28.2 %copy-start.8 = (f32[1024,128]{1,0:T(8,128)S(1)}, f32[1024,128]{1,0:T(8,128)}, u32[]{:S(2)}) copy-start(f32[1024,128]{1,0:T(8,128)} %copy-done.7) | copy-start | bytes 1572868
  182.4 69.1 %copy-start.14 = (f32[1,1152]{1,0:T(1,128)}, f32[1,1152]{1,0:T(1,128)S(1)}, u32[]{:S(2)}) copy-start(f32[1,1152]{1,0:T(1,128)S(1)} %get-tuple-element.50.gp_ref) | copy-start | bytes 13828
  182.5 96.6 %collective-permute-start.5 = (f32[1024,1152]{1,0:T(8,128)}, f32[1024,1152]{1,0:T(8,128)}, u32[]{:S(2)}, u32[]{:S(2)}) collective-permute-start(f32[1024,1152]{1,0:T(8,128)} %get-tuple-element.54.o0), channel_id=1, source_target_pairs={{0,1},{1,0},{2,3},{3,2},{4,5},{5,4},{6,7},{7,6}} | collective-permute-start | bytes 14155784 | tf_op jit(solution)/shard_map/ppermute | solution.py:507
  279.0 10.8 %copy-start.15 = (bf16[1024,1152]{1,0:T(8,128)(2,1)S(1)}, bf16[1024,1152]{1,0:T(8,128)(2,1)}, u32[]{:S(2)}) copy-start(bf16[1024,1152]{1,0:T(8,128)(2,1)} %get-tuple-element.51) | copy-start | bytes 7077892
where the time goes:
time: 291 us
  Pallas kernels  182 us (63%)
  waiting for transfers between devices  90.6 us (31%)
  local copies, waits for them, and re-layouts  7.95 us (3%)
  starting transfers between devices  5.42 us (2%)
  other arithmetic  4.5 us (2%)
    ppermute x6, waiting for transfers between devices, swap(): return lax.ppermute(v, 'cp', [(i, i ^ mask) for i in range(4)])  90.6 us
    pallas_call x1, Pallas kernels, flash_bwd(): pl.pallas_call(bwd_kernel, grid_spec=pltpu.PrefetchScalarGridSpec(num_sca...  68.9 us
    pallas_call x1, Pallas kernels, flash_fwd(): pl.pallas_call(fwd_kernel, grid_spec=pltpu.PrefetchScalarGridSpec(num_sca...  34.8 us
    pallas_call x1, Pallas kernels, post(): pl.pallas_call(post_kernel, grid=(2 * n,), in_specs=[big, big, pl.BlockSp...  28 us
    pallas_call x1, Pallas kernels, final(): pl.pallas_call(final_kernel, in_specs=[ANY] * 13 + [vm, vm], out_specs=[A...  26 us
    pallas_call x2, Pallas kernels, proj(): pl.pallas_call(proj_kernel, grid=(n,), in_specs=[pl.BlockSpec((PR, m), ro...  13.4 us
    pallas_call x1, Pallas kernels, relay(): pl.pallas_call(relay_kernel, grid=(n,), in_specs=[pl.BlockSpec((H, rows,...  10.8 us
  transfers between devices with their start and end apart: 6, of which 2 were waited for; matrix products, arithmetic and copies ran while one was open for 3% of the time, Pallas kernels for 49%

commit v1 on v0

--- a/solution.py
+++ b/solution.py
@@ -89,7 +89,7 @@
     lax.fori_loop(0, NS, body, 0)
 
 
-def fwd_kernel(ids, q_ref, kv0, kv1, kv2, kv3, o_ref, ob_ref, l2_ref, kbuf, vbuf, acc, lacc, sems):
+def fwd_kernel(ids, q_ref, wo_ref, kv0, kv1, kv2, kv3, o_ref, ob_ref, z_ref, l2_ref, kbuf, vbuf, acc, lacc, sems):
     i = pl.program_id(0)
     r = ids[i]
     copies = piece_copies((kv0, kv1, kv2, kv3), kbuf, vbuf, sems)
@@ -121,20 +121,21 @@
         o_ref[:, h*D:(h+1)*D] = o
         ob_ref[:, h*D:(h+1)*D] = o.astype(BF16)
         l2_ref[0, h:h+1, :] = jnp.log2(jnp.sum(la.T, axis=0, keepdims=True))
-
-
-def flash_fwd(ids, q, kvs, us=30):
+    z_ref[...] = dot(ob_ref[...], wo_ref[...]).astype(BF16)
+
+
+def flash_fwd(ids, q, wo, kvs, us=30):
     return pl.pallas_call(
         fwd_kernel,
         grid_spec=pltpu.PrefetchScalarGridSpec(
             num_scalar_prefetch=1, grid=(2*T//CH,),
-            in_specs=[pl.BlockSpec((CH, H*D), row)]+[ANY]*4,
-            out_specs=[pl.BlockSpec((CH, H*D), row), pl.BlockSpec((CH, H*D), row), pl.BlockSpec((1, 8, CH), lambda i, ids: (i, 0, 0))],
+            in_specs=[pl.BlockSpec((CH, H*D), row), whole(wo)]+[ANY]*4,
+            out_specs=[pl.BlockSpec((CH, H*D), row), pl.BlockSpec((CH, H*D), row), pl.BlockSpec((CH, wo.shape[1]), row), pl.BlockSpec((1, 8, CH), lambda i, ids: (i, 0, 0))],
             scratch_shapes=[pltpu.VMEM((NS*CH, D), BF16), pltpu.VMEM((NS*CH, D), BF16), pltpu.VMEM((H, CH, D), F32),
                             pltpu.VMEM((H, CH, 128), F32), pltpu.SemaphoreType.DMA((8,))]),
-        out_shape=[jax.ShapeDtypeStruct((2*T, H*D), F32), jax.ShapeDtypeStruct((2*T, H*D), BF16), jax.ShapeDtypeStruct((4, 8, CH), F32)],
+        out_shape=[jax.ShapeDtypeStruct((2*T, H*D), F32), jax.ShapeDtypeStruct((2*T, H*D), BF16), jax.ShapeDtypeStruct((2*T, wo.shape[1]), BF16), jax.ShapeDtypeStruct((4, 8, CH), F32)],
         compiler_params=params(), cost_estimate=cost(us), name="flash_fwd",
-    )(ids, q, *kvs)
+    )(ids, q, wo, *kvs)
 
 
 def bwd_kernel(ids, q_ref, do_ref, l2_ref, dlt_ref, cl_ref, sl_ref, cr_ref, sr_ref, kv0, kv1, kv2, kv3, dq_ref, own_out, sib_out,
@@ -289,7 +290,7 @@
     )(x, cos, sin, wp, wq, wk, wv, *prev)
 
 
-def post_kernel(ob_ref, o_ref, wp_ref, wo_ref, x_ref, dyl_ref, dyr_ref, y_ref, do_ref, dlt_ref, dwo_ref, dwp_ref, dzs):
+def post_kernel(ob_ref, o_ref, z_ref, wp_ref, wo_ref, x_ref, dyl_ref, dyr_ref, y_ref, do_ref, dlt_ref, dwo_ref, dwp_ref, dzs):
     i = pl.program_id(0)
     left = i < T//BR
     sub = 256
@@ -301,10 +302,8 @@
     gain = 1.0+wp_ref[...]
     def part(u):
         return slice(u*sub, (u+1)*sub)
-    def first(u):
-        return dot(ob_ref[part(u)], wo_ref[...]).astype(BF16)
-    def middle(z, u):
-        z = z.astype(F32)
+    def middle(u):
+        z = z_ref[part(u)].astype(F32)
         rinv = lax.rsqrt(jnp.mean(z*z, axis=-1, keepdims=True)+EPS)
         zh = z*rinv
         dy = jnp.where(left, dyl_ref[part(u)].astype(F32), dyr_ref[part(u)].astype(F32))
@@ -321,19 +320,17 @@
         for h in range(H):
             w = do[:, h*D:(h+1)*D].astype(F32)*o_ref[part(u), h*D:(h+1)*D]
             dlt_ref[0, h:h+1, part(u)] = jnp.sum((w[:, :128]+w[:, 128:]).T, axis=0, keepdims=True)
-    z = first(0)
     dz = None
     for u in range(n):
-        z2 = first(u+1) if u+1 < n else None
-        dz2 = middle(z, u)
+        dz2 = middle(u)
         if dz is not None:
             second(dz, u-1)
-        z, dz = z2, dz2
+        dz = dz2
     second(dz, n-1)
     dwo_ref[...] += dot(ob_ref[...], dzs[...], TN)
 
 
-def post(ob, o, x, dyl, dyr, wp, wo):
+def post(ob, o, z, x, dyl, dyr, wp, wo):
     t, m = x.shape
     n = t//BR
     spec = pl.BlockSpec((BR, m), lambda i: (jnp.minimum(i, n-1), 0))
@@ -341,13 +338,13 @@
     big = pl.BlockSpec((BR, H*D), row)
     return pl.pallas_call(
         post_kernel, grid=(2*n,),
-        in_specs=[big, big, pl.BlockSpec((1, m), const), whole(wo), spec, spec, right],
+        in_specs=[big, big, pl.BlockSpec((BR, m), row), pl.BlockSpec((1, m), const), whole(wo), spec, spec, right],
         out_specs=[spec, big, pl.BlockSpec((1, 8, CH), lambda i: (i, 0, 0)), pl.BlockSpec((H*D, m), const), pl.BlockSpec((1, m), const)],
         scratch_shapes=[pltpu.VMEM((BR, m), BF16)],
         out_shape=[jax.ShapeDtypeStruct((t, m), BF16), jax.ShapeDtypeStruct((2*t, H*D), BF16), jax.ShapeDtypeStruct((4, 8, CH), F32),
                    jax.ShapeDtypeStruct((H*D, m), F32), jax.ShapeDtypeStruct((1, m), F32)],
         compiler_params=params(), cost_estimate=cost(25), name="post",
-    )(ob, o, wp, wo, x, dyl, dyr)
+    )(ob, o, z, wp, wo, x, dyl, dyr)
 
 
 def rope_back(dk, c, s, scale):
@@ -523,8 +520,8 @@
         at, q, kvr = proj(xr, cr, sr, wpre, wq, wk, wv, prev=(at, q), at=2)
         kvrs = swap(kvr, 1)
         kv4 = (kvl, kvr, kvs, kvrs)
-        o, ob, l2 = flash_fwd(ids, q, kv4)
-        y, do, dlt, dwo, dwpost = post(ob, o, x, dy, dyr, wpost, wo)
+        o, ob, z, l2 = flash_fwd(ids, q, wo, kv4)
+        y, do, dlt, dwo, dwpost = post(ob, o, z, x, dy, dyr, wpost, wo)
         dwo_in = swap(dwo, 1)
         dq, own, sib = flash_bwd(ids, q, do, l2, dlt, cl, sl, cr, sr, kv4)
 

time: 291 us -> 291 us (level)
    pallas_call x1, Pallas kernels: 34.8 us -> 39.4 us  [flash_fwd(): pl.pallas_call(fwd_kernel, grid_spec=pltpu.PrefetchScalarGridSpec(num_sca...]
    pallas_call x1, Pallas kernels: 28 us -> 23.7 us  [post(): pl.pallas_call(post_kernel, grid=(2 * n,), in_specs=[big, big, pl.BlockSp...]
  transfers between devices with their start and end apart: 6 -> 6, of which waited for: 2 -> 2; matrix products, arithmetic and copies ran while one was open for 3% -> 3% of each run, Pallas kernels for 49% -> 51%
where the time goes in v1:
time: 291 us
  Pallas kernels  182 us (63%)
  waiting for transfers between devices  90.6 us (31%)
  local copies, waits for them, and re-layouts  7.64 us (3%)
  starting transfers between devices  5.43 us (2%)
  other arithmetic  4.5 us (2%)
    ppermute x6, waiting for transfers between devices, swap(): return lax.ppermute(v, 'cp', [(i, i ^ mask) for i in range(4)])  90.6 us
    pallas_call x1, Pallas kernels, flash_bwd(): pl.pallas_call(bwd_kernel, grid_spec=pltpu.PrefetchScalarGridSpec(num_sca...  69.1 us
    pallas_call x1, Pallas kernels, flash_fwd(): pl.pallas_call(fwd_kernel, grid_spec=pltpu.PrefetchScalarGridSpec(num_sca...  39.4 us
    pallas_call x1, Pallas kernels, final(): pl.pallas_call(final_kernel, in_specs=[ANY] * 13 + [vm, vm], out_specs=[A...  25.7 us
    pallas_call x1, Pallas kernels, post(): pl.pallas_call(post_kernel, grid=(2 * n,), in_specs=[big, big, pl.BlockSp...  23.7 us
    pallas_call x2, Pallas kernels, proj(): pl.pallas_call(proj_kernel, grid=(n,), in_specs=[pl.BlockSpec((PR, m), ro...  13.4 us
    pallas_call x1, Pallas kernels, relay(): pl.pallas_call(relay_kernel, grid=(n,), in_specs=[pl.BlockSpec((H, rows,...  10.8 us
  transfers between devices with their start and end apart: 6, of which 2 were waited for; matrix products, arithmetic and copies ran while one was open for 3% of the time, Pallas kernels for 51%

profile of v1, /device:TPU:0, one launch (start us, length us, event | category | flops | bytes accessed | tf_op | source)
XLA Modules:
  0.0 291.0 jit_solution(13022380752416192126)
XLA Ops:
  0.6 0.0 copy-start.1
  0.6 0.0 copy-start.11
  0.7 0.0 copy-start.10
  0.7 2.8 collective-permute-start
  3.4 0.0 collective-permute-start.4
  3.5 1.7 collective-permute-start.1
  5.2 0.7 convert_element_type.10
  5.9 0.7 reshape.48.refs_3_.wp_ref
  6.6 0.0 copy-start.12
  6.6 2.2 copy.19
  8.8 0.0 copy-start
  8.9 1.9 multiply_sine_fusion.1
  10.8 0.0 copy-start.4
  10.8 0.0 copy-start.5
  10.8 0.0 copy-done.1
  10.8 0.0 copy-done.11
  10.8 0.0 copy-done.10
  10.8 6.7 %proj.2 = (bf16[1152,2048]{1,0:T(8,128)(2,1)}, bf16[2048,1024]{1,0:T(8,128)(2,1)}, bf16[2,1024,256]{2,1,0:T(8,128)(2,1)}) custom-call(bf16[1024,1152]{1,0:T(8,128)(2,1)S(1)} %bitcast.24, f32[1024,128]{1,0:T(8,128)S(1)} %get-tuple-element.67.refs_1_.cl_ref.cl_h, f32[1024,128]{1,0:T(8,128)S(1)} %get-tuple-element.66.refs_2_.sl_ref.sl_h, ...), custom_call_target="tpu_custom_call" | custom-call | flops 320000000 | bytes 1048576 | tf_op jit(solution)/shard_map/proj/pallas_call | solution.py:282
  17.5 0.7 collective-permute-start.2
  18.2 87.8 %collective-permute-done.1 = s32[1024]{0:T(1024)S(1)} collective-permute-done((s32[1024]{0:T(1024)}, s32[1024]{0:T(1024)S(1)}, u32[]{:S(2)}, u32[]{:S(2)}) %collective-permute-start.1) | collective-permute-done | bytes 4128 | tf_op jit(solution)/shard_map/ppermute | solution.py:504
  106.0 1.9 multiply_sine_fusion
  107.8 0.0 copy-start.6
  107.9 0.0 copy-start.8
  107.9 0.0 collective-permute-done.refs_0_
  107.9 0.0 copy-done.12
  107.9 0.0 copy-done
  107.9 0.0 copy-start.15
  107.9 6.7 %proj.3 = (bf16[1152,2048]{1,0:T(8,128)(2,1)}, bf16[2048,1024]{1,0:T(8,128)(2,1)}, bf16[2,1024,256]{2,1,0:T(8,128)(2,1)}) custom-call(bf16[1024,1152]{1,0:T(8,128)(2,1)S(1)} %collective-permute-done.refs_0_, f32[1024,128]{1,0:T(8,128)S(1)} %get-tuple-element.65.refs_1_.cr_ref.cr_h, ...), custom_call_target="tpu_custom_call", output_to_operand_aliasing={{0}: (7, {}), {1}: (8, {})} | custom-call | flops 320000000 | bytes 1048576 | tf_op jit(solution)/shard_map/proj/pallas_call | solution.py:282
  114.6 0.0 copy-done.6
  114.6 0.0 copy-done.8
  114.6 0.1 collective-permute-start.3
  114.7 0.0 copy-done.15
  114.7 0.1 stack.39.ids
  114.8 0.0 collective-permute-done.2.kv2
  114.8 2.8 collective-permute-done.3.kv3
  117.6 0.0 copy-start.3
  117.6 1.7 copy-done.3
  119.3 0.0 copy-start.2
  119.3 39.4 %flash_fwd.1 = (f32[2048,1024]{1,0:T(8,128)}, bf16[2048,1024]{1,0:T(8,128)(2,1)}, bf16[2048,1152]{1,0:T(8,128)(2,1)}, f32[4,8,512]{2,1,0:T(8,128)S(1)}) custom-call(s32[12]{0:T(128)S(1)} %stack.39.ids, bf16[2048,1024]{1,0:T(8,128)(2,1)} %get-tuple-element.39.q_ref, bf16[1024,1152]{1,0:T(8,128)(2,1)S(1)} %bitcast.29, ...), custom_call_target="tpu_custom_call" | custom-call | flops 1200000000 | bytes 1048576 | tf_op jit(solution)/shard_map/flash_fwd/pallas_call | solution.py:128
  158.7 0.0 collective-permute-done.4.dyr_ref
  158.7 0.0 copy-done.2
  158.7 0.0 copy-start.7
  158.7 0.0 copy-start.9
  158.7 23.7 %post.1 = (bf16[1024,1152]{1,0:T(8,128)(2,1)}, bf16[2048,1024]{1,0:T(8,128)(2,1)}, f32[4,8,512]{2,1,0:T(8,128)S(1)}, f32[1024,1152]{1,0:T(8,128)}, f32[1,1152]{1,0:T(1,128)S(1)}) custom-call(bf16[2048,1024]{1,0:T(8,128)(2,1)} %get-tuple-element.41.ob_ref, f32[2048,1024]{1,0:T(8,128)} %get-tuple-element.42.o_ref, bf16[2048,1152]{1,0:T(8,128)(2,1)} %get-tuple-element.43.z_ref, ...), custom_call_target="tpu_custom_call" | custom-call | flops 1000000000 | bytes 1048576 | tf_op jit(solution)/shard_map/post/pallas_call | solution.py:339
  182.5 0.0 copy-start.13
  182.5 0.2 collective-permute-start.5
  182.6 0.0 copy-done.4
  182.6 0.0 copy-done.5
  182.6 0.0 copy-done.7
  182.6 0.0 copy-done.9
  182.6 69.1 %flash_bwd.1 = (bf16[2048,1024]{1,0:T(8,128)(2,1)}, f32[2,2048,256]{2,1,0:T(8,128)}, f32[2,2048,256]{2,1,0:T(8,128)}) custom-call(s32[12]{0:T(128)S(1)} %stack.39.ids, bf16[2048,1024]{1,0:T(8,128)(2,1)} %get-tuple-element.39.q_ref, bf16[2048,1024]{1,0:T(8,128)(2,1)} %get-tuple-element.46.do_ref, f32[4,8,512]{2,1,0:T(8,128)S(1)} %get-tuple-element.47.l2_ref, ...), custom_call_target="tpu_custom_call" | custom-call | flops 2800000000 | bytes 1048576 | tf_op jit(solution)/shard_map/flash_bwd/pallas_call | solution.py:240
  251.7 0.0 copy-done.13
  251.7 25.7 %final.1 = (f32[4,1152,256]{2,1,0:T(8,128)}, f32[1152,512]{1,0:T(8,128)}, bf16[1024,1152]{1,0:T(8,128)(2,1)}, f32[8,1152]{1,0:T(8,128)}) custom-call(bf16[1152,2048]{1,0:T(8,128)(2,1)} %get-tuple-element.45.at_h, bf16[2048,1024]{1,0:T(8,128)(2,1)} %get-tuple-element.49.dq_h, f32[2,2048,256]{2,1,0:T(8,128)} %get-tuple-element.50.own_h, ...), custom_call_target="tpu_custom_call" | custom-call | flops 800000000 | bytes 1048576 | tf_op jit(solution)/shard_map/final/pallas_call | solution.py:449
  277.4 1.5 slice_reduce_fusion
  278.9 0.0 collective-permute-done.5.o1
  278.9 0.0 copy-start.14
  278.9 10.8 %relay.1 = (f32[1152,4,256]{2,1,0:T(4,128)}, f32[1152,1,256]{2,1,0:T(1,128)}, f32[1152,1,256]{2,1,0:T(1,128)}, f32[1024,1152]{1,0:T(8,128)}) custom-call(f32[4,1152,256]{2,1,0:T(8,128)} %get-tuple-element.54.q_ref, f32[1152,512]{1,0:T(8,128)} %get-tuple-element.55.kv_ref, f32[1024,1152]{1,0:T(8,128)} %get-tuple-element.56.o0, ...), custom_call_target="tpu_custom_call" | custom-call | flops 360000000 | bytes 1048576 | tf_op jit(solution)/shard_map/relay/pallas_call | solution.py:475
  289.6 0.0 copy-done.14
  289.6 1.4 copy.23
  (3 shorter events, 0.0 us)
Async XLA Ops:
  0.6 10.2 %copy-start.1 = (bf16[1,1024,1152]{2,1,0:T(8,128)(2,1)S(1)}, bf16[1,1024,1152]{2,1,0:T(8,128)(2,1)}, u32[]{:S(2)}) copy-start(bf16[1,1024,1152]{2,1,0:T(8,128)(2,1)} %param.9) | copy-start | bytes 7077892
  0.6 10.1 %copy-start.11 = (bf16[1152,1,256]{2,0,1:T(8,128)(2,1)S(1)}, bf16[1152,1,256]{2,0,1:T(8,128)(2,1)}, u32[]{:S(2)}) copy-start(bf16[1152,1,256]{2,0,1:T(8,128)(2,1)} %param.14) | copy-start | bytes 1769476
  0.7 10.1 %copy-start.10 = (bf16[1152,1,256]{2,0,1:T(8,128)(2,1)S(1)}, bf16[1152,1,256]{2,0,1:T(8,128)(2,1)}, u32[]{:S(2)}) copy-start(bf16[1152,1,256]{2,0,1:T(8,128)(2,1)} %param.13) | copy-start | bytes 1769476
  0.7 107.2 %collective-permute-start = (bf16[1024,1152]{1,0:T(8,128)(2,1)}, bf16[1024,1152]{1,0:T(8,128)(2,1)S(1)}, u32[]{:S(2)}, u32[]{:S(2)}) collective-permute-start(bf16[1024,1152]{1,0:T(8,128)(2,1)} %bitcast.22), channel_id=1, source_target_pairs={{0,3},{1,2},{2,1},{3,0},{4,7},{5,6},{6,5},{7,4}} | collective-permute-start | bytes 7077896 | tf_op jit(solution)/shard_map/ppermute | solution.py:504
  3.4 155.2 %collective-permute-start.4 = (bf16[1024,1152]{1,0:T(8,128)(2,1)}, bf16[1024,1152]{1,0:T(8,128)(2,1)}, u32[]{:S(2)}, u32[]{:S(2)}) collective-permute-start(bf16[1024,1152]{1,0:T(8,128)(2,1)} %bitcast.26), channel_id=1, source_target_pairs={{0,3},{1,2},{2,1},{3,0},{4,7},{5,6},{6,5},{7,4}} | collective-permute-start | bytes 7077896 | tf_op jit(solution)/shard_map/ppermute | solution.py:504
  3.5 102.5 %collective-permute-start.1 = (s32[1024]{0:T(1024)}, s32[1024]{0:T(1024)S(1)}, u32[]{:S(2)}, u32[]{:S(2)}) collective-permute-start(s32[1024]{0:T(1024)} %bitcast.39), channel_id=1, source_target_pairs={{0,3},{1,2},{2,1},{3,0},{4,7},{5,6},{6,5},{7,4}} | collective-permute-start | bytes 12296 | tf_op jit(solution)/shard_map/ppermute | solution.py:504
  6.6 101.3 %copy-start.12 = (f32[1,1152]{1,0:T(1,128)}, f32[1,1152]{1,0:T(1,128)S(1)}, u32[]{:S(2)}) copy-start(f32[1,1152]{1,0:T(1,128)S(1)} %reshape.48.refs_3_.wp_ref) | copy-start | bytes 13828
  8.8 99.0 %copy-start = (bf16[144,8,4,256]{3,1,2,0:T(8,128)(2,1)}, bf16[144,8,4,256]{3,1,2,0:T(8,128)(2,1)S(1)}, u32[]{:S(2)}) copy-start(bf16[144,8,4,256]{3,1,2,0:T(8,128)(2,1)S(1)} %copy.19) | copy-start | bytes 7077892
  10.8 171.9 %copy-start.4 = (f32[1024,128]{1,0:T(8,128)}, f32[1024,128]{1,0:T(8,128)S(1)}, u32[]{:S(2)}) copy-start(f32[1024,128]{1,0:T(8,128)S(1)} %get-tuple-element.66.refs_2_.sl_ref.sl_h) | copy-start | bytes 1572868
  10.8 171.9 %copy-start.5 = (f32[1024,128]{1,0:T(8,128)}, f32[1024,128]{1,0:T(8,128)S(1)}, u32[]{:S(2)}) copy-start(f32[1024,128]{1,0:T(8,128)S(1)} %get-tuple-element.67.refs_1_.cl_ref.cl_h) | copy-start | bytes 1572868
  17.5 97.3 %collective-permute-start.2 = (bf16[2,1024,256]{2,1,0:T(8,128)(2,1)}, bf16[2,1024,256]{2,1,0:T(8,128)(2,1)}, u32[]{:S(2)}, u32[]{:S(2)}) collective-permute-start(bf16[2,1024,256]{2,1,0:T(8,128)(2,1)} %get-tuple-element.35.kv0), channel_id=1, source_target_pairs={{0,1},{1,0},{2,3},{3,2},{4,5},{5,4},{6,7},{7,6}} | collective-permute-start | bytes 3145736 | tf_op jit(solution)/shard_map/ppermute | solution.py:504
  107.8 6.8 %copy-start.6 = (f32[1024,128]{1,0:T(8,128)}, f32[1024,128]{1,0:T(8,128)S(1)}, u32[]{:S(2)}) copy-start(f32[1024,128]{1,0:T(8,128)S(1)} %get-tuple-element.64.refs_2_.sr_ref.sr_h) | copy-start | bytes 1572868
  107.9 6.8 %copy-start.8 = (f32[1024,128]{1,0:T(8,128)}, f32[1024,128]{1,0:T(8,128)S(1)}, u32[]{:S(2)}) copy-start(f32[1024,128]{1,0:T(8,128)S(1)} %get-tuple-element.65.refs_1_.cr_ref.cr_h) | copy-start | bytes 1572868
  107.9 6.8 %copy-start.15 = (f32[1152]{0:T(1024)S(1)}, f32[1152]{0:T(1024)}, u32[]{:S(2)}) copy-start(f32[1152]{0:T(1024)} %param.17) | copy-start | bytes 13828
  114.6 3.0 %collective-permute-start.3 = (bf16[2,1024,256]{2,1,0:T(8,128)(2,1)}, bf16[2,1024,256]{2,1,0:T(8,128)(2,1)}, u32[]{:S(2)}, u32[]{:S(2)}) collective-permute-start(bf16[2,1024,256]{2,1,0:T(8,128)(2,1)} %get-tuple-element.40.kv1), channel_id=1, source_target_pairs={{0,1},{1,0},{2,3},{3,2},{4,5},{5,4},{6,7},{7,6}} | collective-permute-start | bytes 3145736 | tf_op jit(solution)/shard_map/ppermute | solution.py:504
  117.6 1.7 copy-start.3
  119.3 39.4 %copy-start.2 = (bf16[1,1024,1152]{2,1,0:T(8,128)(2,1)S(1)}, bf16[1,1024,1152]{2,1,0:T(8,128)(2,1)}, u32[]{:S(2)}) copy-start(bf16[1,1024,1152]{2,1,0:T(8,128)(2,1)} %param.11) | copy-start | bytes 7077892
  158.7 23.9 %copy-start.7 = (f32[1024,128]{1,0:T(8,128)S(1)}, f32[1024,128]{1,0:T(8,128)}, u32[]{:S(2)}) copy-start(f32[1024,128]{1,0:T(8,128)} %copy-done.6) | copy-start | bytes 1572868
  158.7 23.9 %copy-start.9 = (f32[1024,128]{1,0:T(8,128)S(1)}, f32[1024,128]{1,0:T(8,128)}, u32[]{:S(2)}) copy-start(f32[1024,128]{1,0:T(8,128)} %copy-done.8) | copy-start | bytes 1572868
  182.5 69.2 %copy-start.13 = (f32[1,1152]{1,0:T(1,128)}, f32[1,1152]{1,0:T(1,128)S(1)}, u32[]{:S(2)}) copy-start(f32[1,1152]{1,0:T(1,128)S(1)} %get-tuple-element.52.gp_ref) | copy-start | bytes 13828
  182.5 96.4 %collective-permute-start.5 = (f32[1024,1152]{1,0:T(8,128)}, f32[1024,1152]{1,0:T(8,128)}, u32[]{:S(2)}, u32[]{:S(2)}) collective-permute-start(f32[1024,1152]{1,0:T(8,128)} %get-tuple-element.56.o0), channel_id=1, source_target_pairs={{0,1},{1,0},{2,3},{3,2},{4,5},{5,4},{6,7},{7,6}} | collective-permute-start | bytes 14155784 | tf_op jit(solution)/shard_map/ppermute | solution.py:504
  278.9 10.8 %copy-start.14 = (bf16[1024,1152]{1,0:T(8,128)(2,1)S(1)}, bf16[1024,1152]{1,0:T(8,128)(2,1)}, u32[]{:S(2)}) copy-start(bf16[1024,1152]{1,0:T(8,128)(2,1)} %get-tuple-element.53) | copy-start | bytes 7077892

commit v2 on v1

--- a/solution.py
+++ b/solution.py
@@ -134,7 +134,7 @@
             scratch_shapes=[pltpu.VMEM((NS*CH, D), BF16), pltpu.VMEM((NS*CH, D), BF16), pltpu.VMEM((H, CH, D), F32),
                             pltpu.VMEM((H, CH, 128), F32), pltpu.SemaphoreType.DMA((8,))]),
         out_shape=[jax.ShapeDtypeStruct((2*T, H*D), F32), jax.ShapeDtypeStruct((2*T, H*D), BF16), jax.ShapeDtypeStruct((2*T, wo.shape[1]), BF16), jax.ShapeDtypeStruct((4, 8, CH), F32)],
-        compiler_params=params(), cost_estimate=cost(us), name="flash_fwd",
+        compiler_params=params(54 << 20), cost_estimate=cost(us), name="flash_fwd",
     )(ids, q, wo, *kvs)
 
 
@@ -467,7 +467,7 @@
     do_ref[...] = o0[...]+o1[...]
 
 
-def relay(q, kv, o0, o1, n=4):
+def relay(q, kv, o0, o1, n=2):
     m = kv.shape[0]
     rows = m//n
     out = lambda e: pl.BlockSpec((rows, e, D), lambda i: (i, 0, 0))

time: 291 us -> 289 us (level)
  no operation moved by 1% of the time
where the time goes in v2:
time: 289 us; the launch traced here: 288 us
  Pallas kernels  181 us (63%)
  waiting for transfers between devices  90 us (31%)
  local copies, waits for them, and re-layouts  6.57 us (2%)
  starting transfers between devices  5.43 us (2%)
  other arithmetic  4.5 us (2%)
    ppermute x6, waiting for transfers between devices, swap(): return lax.ppermute(v, 'cp', [(i, i ^ mask) for i in range(4)])  90 us
    pallas_call x1, Pallas kernels, flash_bwd(): pl.pallas_call(bwd_kernel, grid_spec=pltpu.PrefetchScalarGridSpec(num_sca...  69 us
    pallas_call x1, Pallas kernels, flash_fwd(): pl.pallas_call(fwd_kernel, grid_spec=pltpu.PrefetchScalarGridSpec(num_sca...  39.6 us
    pallas_call x1, Pallas kernels, final(): pl.pallas_call(final_kernel, in_specs=[ANY] * 13 + [vm, vm], out_specs=[A...  25.7 us
    pallas_call x1, Pallas kernels, post(): pl.pallas_call(post_kernel, grid=(2 * n,), in_specs=[big, big, pl.BlockSp...  23.3 us
    pallas_call x2, Pallas kernels, proj(): pl.pallas_call(proj_kernel, grid=(n,), in_specs=[pl.BlockSpec((PR, m), ro...  13.4 us
    pallas_call x1, Pallas kernels, relay(): pl.pallas_call(relay_kernel, grid=(n,), in_specs=[pl.BlockSpec((H, rows,...  9.87 us
  transfers between devices with their start and end apart: 6, of which 2 were waited for; matrix products, arithmetic and copies ran while one was open for 3% of the time, Pallas kernels for 51%

profile of v2, /device:TPU:0, one launch (start us, length us, event | category | flops | bytes accessed | tf_op | source)
XLA Modules:
  0.0 288.3 jit_solution(12082222178137770485)
XLA Ops:
  0.6 0.0 copy-start.1
  0.6 0.0 copy-start.11
  0.7 0.0 copy-start.10
  0.7 2.8 collective-permute-start
  3.4 0.0 collective-permute-start.4
  3.5 1.7 collective-permute-start.1
  5.2 0.7 convert_element_type.10
  5.9 0.7 reshape.48.refs_3_.wp_ref
  6.6 0.0 copy-start.12
  6.6 2.2 copy.19
  8.8 0.0 copy-start
  8.9 1.9 multiply_sine_fusion.1
  10.8 0.0 copy-start.4
  10.8 0.0 copy-start.5
  10.8 0.0 copy-done.1
  10.8 0.0 copy-done.11
  10.8 0.0 copy-done.10
  10.8 6.7 %proj.2 = (bf16[1152,2048]{1,0:T(8,128)(2,1)}, bf16[2048,1024]{1,0:T(8,128)(2,1)}, bf16[2,1024,256]{2,1,0:T(8,128)(2,1)}) custom-call(bf16[1024,1152]{1,0:T(8,128)(2,1)S(1)} %bitcast.24, f32[1024,128]{1,0:T(8,128)S(1)} %get-tuple-element.67.refs_1_.cl_ref.cl_h, f32[1024,128]{1,0:T(8,128)S(1)} %get-tuple-element.66.refs_2_.sl_ref.sl_h, ...), custom_call_target="tpu_custom_call" | custom-call | flops 320000000 | bytes 1048576 | tf_op jit(solution)/shard_map/proj/pallas_call | solution.py:282
  17.5 0.7 collective-permute-start.2
  18.2 87.8 %collective-permute-done.1 = s32[1024]{0:T(1024)S(1)} collective-permute-done((s32[1024]{0:T(1024)}, s32[1024]{0:T(1024)S(1)}, u32[]{:S(2)}, u32[]{:S(2)}) %collective-permute-start.1) | collective-permute-done | bytes 4128 | tf_op jit(solution)/shard_map/ppermute | solution.py:504
  106.0 1.9 multiply_sine_fusion
  107.8 0.0 copy-start.6
  107.9 0.0 copy-start.8
  107.9 0.0 collective-permute-done.refs_0_
  107.9 0.0 copy-done.12
  107.9 0.0 copy-done
  107.9 0.0 copy-start.17
  107.9 6.7 %proj.3 = (bf16[1152,2048]{1,0:T(8,128)(2,1)}, bf16[2048,1024]{1,0:T(8,128)(2,1)}, bf16[2,1024,256]{2,1,0:T(8,128)(2,1)}) custom-call(bf16[1024,1152]{1,0:T(8,128)(2,1)S(1)} %collective-permute-done.refs_0_, f32[1024,128]{1,0:T(8,128)S(1)} %get-tuple-element.65.refs_1_.cr_ref.cr_h, ...), custom_call_target="tpu_custom_call", output_to_operand_aliasing={{0}: (7, {}), {1}: (8, {})} | custom-call | flops 320000000 | bytes 1048576 | tf_op jit(solution)/shard_map/proj/pallas_call | solution.py:282
  114.6 0.0 copy-done.6
  114.6 0.0 copy-done.8
  114.6 0.1 collective-permute-start.3
  114.7 0.0 copy-done.17
  114.7 0.7 stack.39.ids
  115.4 0.0 collective-permute-done.2.kv2
  115.4 2.2 collective-permute-done.3.kv3
  117.6 0.0 copy-start.2
  117.6 0.0 copy-start.3
  117.6 39.6 %flash_fwd.1 = (f32[2048,1024]{1,0:T(8,128)}, bf16[2048,1024]{1,0:T(8,128)(2,1)}, bf16[2048,1152]{1,0:T(8,128)(2,1)}, f32[4,8,512]{2,1,0:T(8,128)}) custom-call(s32[12]{0:T(128)} %stack.39.ids, bf16[2048,1024]{1,0:T(8,128)(2,1)} %get-tuple-element.39.q_ref, bf16[1024,1152]{1,0:T(8,128)(2,1)} %bitcast.29, bf16[2,1024,256]{2,1,0:T(8,128)(2,1)} %get-tuple-element.35.kv0, ...), custom_call_target="tpu_custom_call" | custom-call | flops 1200000000 | bytes 1048576 | tf_op jit(solution)/shard_map/flash_fwd/pallas_call | solution.py:128
  157.2 0.0 collective-permute-done.4.dyr_ref
  157.2 0.0 copy-done.2
  157.3 0.0 copy-done.3
  157.3 0.0 copy-start.7
  157.3 0.0 copy-start.9
  157.3 0.0 copy-start.13
  157.3 0.0 copy-start.15
  157.3 23.3 %post.1 = (bf16[1024,1152]{1,0:T(8,128)(2,1)}, bf16[2048,1024]{1,0:T(8,128)(2,1)}, f32[4,8,512]{2,1,0:T(8,128)S(1)}, f32[1024,1152]{1,0:T(8,128)}, f32[1,1152]{1,0:T(1,128)S(1)}) custom-call(bf16[2048,1024]{1,0:T(8,128)(2,1)} %get-tuple-element.41.ob_ref, f32[2048,1024]{1,0:T(8,128)} %get-tuple-element.42.o_ref, bf16[2048,1152]{1,0:T(8,128)(2,1)} %get-tuple-element.43.z_ref, ...), custom_call_target="tpu_custom_call" | custom-call | flops 1000000000 | bytes 1048576 | tf_op jit(solution)/shard_map/post/pallas_call | solution.py:339
  180.6 0.0 copy-start.14
  180.6 0.2 collective-permute-start.5
  180.7 0.0 copy-done.4
  180.7 0.0 copy-done.5
  180.7 0.0 copy-done.7
  180.7 0.0 copy-done.9
  180.7 0.0 copy-done.13
  180.8 0.0 copy-done.15
  180.8 69.0 %flash_bwd.1 = (bf16[2048,1024]{1,0:T(8,128)(2,1)}, f32[2,2048,256]{2,1,0:T(8,128)}, f32[2,2048,256]{2,1,0:T(8,128)}) custom-call(s32[12]{0:T(128)S(1)} %copy-done.15, bf16[2048,1024]{1,0:T(8,128)(2,1)} %get-tuple-element.39.q_ref, bf16[2048,1024]{1,0:T(8,128)(2,1)} %get-tuple-element.46.do_ref, f32[4,8,512]{2,1,0:T(8,128)S(1)} %copy-done.13, ...), custom_call_target="tpu_custom_call" | custom-call | flops 2800000000 | bytes 1048576 | tf_op jit(solution)/shard_map/flash_bwd/pallas_call | solution.py:240
  249.7 0.0 copy-done.14
  249.7 25.7 %final.1 = (f32[4,1152,256]{2,1,0:T(8,128)}, f32[1152,512]{1,0:T(8,128)}, bf16[1024,1152]{1,0:T(8,128)(2,1)}, f32[8,1152]{1,0:T(8,128)}) custom-call(bf16[1152,2048]{1,0:T(8,128)(2,1)} %get-tuple-element.45.at_h, bf16[2048,1024]{1,0:T(8,128)(2,1)} %get-tuple-element.49.dq_h, f32[2,2048,256]{2,1,0:T(8,128)} %get-tuple-element.50.own_h, ...), custom_call_target="tpu_custom_call" | custom-call | flops 800000000 | bytes 1048576 | tf_op jit(solution)/shard_map/final/pallas_call | solution.py:449
  275.5 1.5 slice_reduce_fusion
  277.0 0.0 collective-permute-done.5.o1
  277.0 0.0 copy-start.16
  277.0 9.9 %relay.1 = (f32[1152,4,256]{2,1,0:T(4,128)}, f32[1152,1,256]{2,1,0:T(1,128)}, f32[1152,1,256]{2,1,0:T(1,128)}, f32[1024,1152]{1,0:T(8,128)}) custom-call(f32[4,1152,256]{2,1,0:T(8,128)} %get-tuple-element.54.q_ref, f32[1152,512]{1,0:T(8,128)} %get-tuple-element.55.kv_ref, f32[1024,1152]{1,0:T(8,128)} %get-tuple-element.56.o0, ...), custom_call_target="tpu_custom_call" | custom-call | flops 360000000 | bytes 1048576 | tf_op jit(solution)/shard_map/relay/pallas_call | solution.py:475
  286.8 0.0 copy-done.16
  286.9 1.4 copy.23
  (3 shorter events, 0.0 us)
Async XLA Ops:
  0.6 10.2 %copy-start.1 = (bf16[1,1024,1152]{2,1,0:T(8,128)(2,1)S(1)}, bf16[1,1024,1152]{2,1,0:T(8,128)(2,1)}, u32[]{:S(2)}) copy-start(bf16[1,1024,1152]{2,1,0:T(8,128)(2,1)} %param.9) | copy-start | bytes 7077892
  0.6 10.1 %copy-start.11 = (bf16[1152,1,256]{2,0,1:T(8,128)(2,1)S(1)}, bf16[1152,1,256]{2,0,1:T(8,128)(2,1)}, u32[]{:S(2)}) copy-start(bf16[1152,1,256]{2,0,1:T(8,128)(2,1)} %param.14) | copy-start | bytes 1769476
  0.7 10.1 %copy-start.10 = (bf16[1152,1,256]{2,0,1:T(8,128)(2,1)S(1)}, bf16[1152,1,256]{2,0,1:T(8,128)(2,1)}, u32[]{:S(2)}) copy-start(bf16[1152,1,256]{2,0,1:T(8,128)(2,1)} %param.13) | copy-start | bytes 1769476
  0.7 107.2 %collective-permute-start = (bf16[1024,1152]{1,0:T(8,128)(2,1)}, bf16[1024,1152]{1,0:T(8,128)(2,1)S(1)}, u32[]{:S(2)}, u32[]{:S(2)}) collective-permute-start(bf16[1024,1152]{1,0:T(8,128)(2,1)} %bitcast.22), channel_id=1, source_target_pairs={{0,3},{1,2},{2,1},{3,0},{4,7},{5,6},{6,5},{7,4}} | collective-permute-start | bytes 7077896 | tf_op jit(solution)/shard_map/ppermute | solution.py:504
  3.4 153.8 %collective-permute-start.4 = (bf16[1024,1152]{1,0:T(8,128)(2,1)}, bf16[1024,1152]{1,0:T(8,128)(2,1)}, u32[]{:S(2)}, u32[]{:S(2)}) collective-permute-start(bf16[1024,1152]{1,0:T(8,128)(2,1)} %bitcast.26), channel_id=1, source_target_pairs={{0,3},{1,2},{2,1},{3,0},{4,7},{5,6},{6,5},{7,4}} | collective-permute-start | bytes 7077896 | tf_op jit(solution)/shard_map/ppermute | solution.py:504
  3.5 102.5 %collective-permute-start.1 = (s32[1024]{0:T(1024)}, s32[1024]{0:T(1024)S(1)}, u32[]{:S(2)}, u32[]{:S(2)}) collective-permute-start(s32[1024]{0:T(1024)} %bitcast.39), channel_id=1, source_target_pairs={{0,3},{1,2},{2,1},{3,0},{4,7},{5,6},{6,5},{7,4}} | collective-permute-start | bytes 12296 | tf_op jit(solution)/shard_map/ppermute | solution.py:504
  6.6 101.3 %copy-start.12 = (f32[1,1152]{1,0:T(1,128)}, f32[1,1152]{1,0:T(1,128)S(1)}, u32[]{:S(2)}) copy-start(f32[1,1152]{1,0:T(1,128)S(1)} %reshape.48.refs_3_.wp_ref) | copy-start | bytes 13828
  8.8 99.0 %copy-start = (bf16[144,8,4,256]{3,1,2,0:T(8,128)(2,1)}, bf16[144,8,4,256]{3,1,2,0:T(8,128)(2,1)S(1)}, u32[]{:S(2)}) copy-start(bf16[144,8,4,256]{3,1,2,0:T(8,128)(2,1)S(1)} %copy.19) | copy-start | bytes 7077892
  10.8 170.0 %copy-start.4 = (f32[1024,128]{1,0:T(8,128)}, f32[1024,128]{1,0:T(8,128)S(1)}, u32[]{:S(2)}) copy-start(f32[1024,128]{1,0:T(8,128)S(1)} %get-tuple-element.66.refs_2_.sl_ref.sl_h) | copy-start | bytes 1572868
  10.8 170.0 %copy-start.5 = (f32[1024,128]{1,0:T(8,128)}, f32[1024,128]{1,0:T(8,128)S(1)}, u32[]{:S(2)}) copy-start(f32[1024,128]{1,0:T(8,128)S(1)} %get-tuple-element.67.refs_1_.cl_ref.cl_h) | copy-start | bytes 1572868
  17.5 97.9 %collective-permute-start.2 = (bf16[2,1024,256]{2,1,0:T(8,128)(2,1)}, bf16[2,1024,256]{2,1,0:T(8,128)(2,1)}, u32[]{:S(2)}, u32[]{:S(2)}) collective-permute-start(bf16[2,1024,256]{2,1,0:T(8,128)(2,1)} %get-tuple-element.35.kv0), channel_id=1, source_target_pairs={{0,1},{1,0},{2,3},{3,2},{4,5},{5,4},{6,7},{7,6}} | collective-permute-start | bytes 3145736 | tf_op jit(solution)/shard_map/ppermute | solution.py:504
  107.8 6.8 %copy-start.6 = (f32[1024,128]{1,0:T(8,128)}, f32[1024,128]{1,0:T(8,128)S(1)}, u32[]{:S(2)}) copy-start(f32[1024,128]{1,0:T(8,128)S(1)} %get-tuple-element.64.refs_2_.sr_ref.sr_h) | copy-start | bytes 1572868
  107.9 6.8 %copy-start.8 = (f32[1024,128]{1,0:T(8,128)}, f32[1024,128]{1,0:T(8,128)S(1)}, u32[]{:S(2)}) copy-start(f32[1024,128]{1,0:T(8,128)S(1)} %get-tuple-element.65.refs_1_.cr_ref.cr_h) | copy-start | bytes 1572868
  107.9 6.8 %copy-start.17 = (f32[1152]{0:T(1024)S(1)}, f32[1152]{0:T(1024)}, u32[]{:S(2)}) copy-start(f32[1152]{0:T(1024)} %param.17) | copy-start | bytes 13828
  114.6 3.0 %collective-permute-start.3 = (bf16[2,1024,256]{2,1,0:T(8,128)(2,1)}, bf16[2,1024,256]{2,1,0:T(8,128)(2,1)}, u32[]{:S(2)}, u32[]{:S(2)}) collective-permute-start(bf16[2,1024,256]{2,1,0:T(8,128)(2,1)} %get-tuple-element.40.kv1), channel_id=1, source_target_pairs={{0,1},{1,0},{2,3},{3,2},{4,5},{5,4},{6,7},{7,6}} | collective-permute-start | bytes 3145736 | tf_op jit(solution)/shard_map/ppermute | solution.py:504
  117.6 39.6 %copy-start.2 = (bf16[1,1024,1152]{2,1,0:T(8,128)(2,1)S(1)}, bf16[1,1024,1152]{2,1,0:T(8,128)(2,1)}, u32[]{:S(2)}) copy-start(bf16[1,1024,1152]{2,1,0:T(8,128)(2,1)} %param.11) | copy-start | bytes 7077892
  117.6 39.6 %copy-start.3 = (bf16[4,256,1152]{2,1,0:T(8,128)(2,1)S(1)}, bf16[4,256,1152]{2,1,0:T(8,128)(2,1)}, u32[]{:S(2)}) copy-start(bf16[4,256,1152]{2,1,0:T(8,128)(2,1)} %param.15) | copy-start | bytes 7077892
  157.3 23.5 %copy-start.7 = (f32[1024,128]{1,0:T(8,128)S(1)}, f32[1024,128]{1,0:T(8,128)}, u32[]{:S(2)}) copy-start(f32[1024,128]{1,0:T(8,128)} %copy-done.6) | copy-start | bytes 1572868
  157.3 23.5 %copy-start.9 = (f32[1024,128]{1,0:T(8,128)S(1)}, f32[1024,128]{1,0:T(8,128)}, u32[]{:S(2)}) copy-start(f32[1024,128]{1,0:T(8,128)} %copy-done.8) | copy-start | bytes 1572868
  157.3 23.5 %copy-start.13 = (f32[4,8,512]{2,1,0:T(8,128)S(1)}, f32[4,8,512]{2,1,0:T(8,128)}, u32[]{:S(2)}) copy-start(f32[4,8,512]{2,1,0:T(8,128)} %get-tuple-element.47.l2_ref) | copy-start | bytes 196612
  157.3 23.5 %copy-start.15 = (s32[12]{0:T(128)S(1)}, s32[12]{0:T(128)}, u32[]{:S(2)}) copy-start(s32[12]{0:T(128)} %stack.39.ids) | copy-start | bytes 148
  180.6 69.2 %copy-start.14 = (f32[1,1152]{1,0:T(1,128)}, f32[1,1152]{1,0:T(1,128)S(1)}, u32[]{:S(2)}) copy-start(f32[1,1152]{1,0:T(1,128)S(1)} %get-tuple-element.52.gp_ref) | copy-start | bytes 13828
  180.6 96.4 %collective-permute-start.5 = (f32[1024,1152]{1,0:T(8,128)}, f32[1024,1152]{1,0:T(8,128)}, u32[]{:S(2)}, u32[]{:S(2)}) collective-permute-start(f32[1024,1152]{1,0:T(8,128)} %get-tuple-element.56.o0), channel_id=1, source_target_pairs={{0,1},{1,0},{2,3},{3,2},{4,5},{5,4},{6,7},{7,6}} | collective-permute-start | bytes 14155784 | tf_op jit(solution)/shard_map/ppermute | solution.py:504
  277.0 9.9 %copy-start.16 = (bf16[1024,1152]{1,0:T(8,128)(2,1)S(1)}, bf16[1024,1152]{1,0:T(8,128)(2,1)}, u32[]{:S(2)}) copy-start(bf16[1024,1152]{1,0:T(8,128)(2,1)} %get-tuple-element.53) | copy-start | bytes 7077892
